TPU v7x, 32 devices: a whole 2x2x4 slice. The times are simulated.
32 devices in a mesh: dp: 4 (over z), expert: 8 (over y, x, core).
Axes of the slice: x: 2, y: 2, z: 4, core: 2. Of those that a mesh axis runs over, the one named last changes fastest.
Arguments:
- tokens: bfloat16 [2, 12288, 768], P(None, ('dp', 'expert')), may hold values from -6 to 6
- cotangent: bfloat16 [2, 12288, 768], P(None, ('dp', 'expert')), may hold values from -6 to 6
- token_ids: int32 [2, 12288], P(None, ('dp', 'expert')), may hold values from 0 to 8007, as said below
- hash_table: int32 [8008], replicated, may hold values from 0 to 7, as said below
- segment_ids: int32 [2, 12288], P(None, ('dp', 'expert')), may hold values from 0 to 1, as said below
- query_weight: bfloat16 [768, 768], replicated, may hold values from -0.21875 to 0.21875
- key_weight: bfloat16 [768, 768], replicated, may hold values from -0.21875 to 0.21875
- value_weight: bfloat16 [768, 768], replicated, may hold values from -0.21875 to 0.21875
- output_weight: bfloat16 [768, 768], replicated, may hold values from -2.5 to 2.5
- gain_attn: float32 [768], replicated, may hold values from 0.5 to 1.5
- gain_ffn: float32 [768], replicated, may hold values from 0.5 to 1.5
- expert_in: bfloat16 [8, 768, 3072], P('expert'), may hold values from -0.21875 to 0.21875
- expert_out: bfloat16 [8, 3072, 768], P('expert'), may hold values from -0.109375 to 0.109375
Outputs:
- block_out: bfloat16 [2, 12288, 768], P(None, ('dp', 'expert'))
- grad_tokens: bfloat16 [2, 12288, 768], P(None, ('dp', 'expert'))
- grad_query: float32 [768, 768], replicated
- grad_key: float32 [768, 768], replicated
- grad_value: float32 [768, 768], replicated
- grad_output: float32 [768, 768], replicated
- grad_gain_attn: float32 [768], replicated
- grad_gain_ffn: float32 [768], replicated
- grad_expert_in: float32 [8, 768, 3072], P('expert')
- grad_expert_out: float32 [8, 3072, 768], P('expert')
Inputs may be any that keep to these rules, and one draw needn't show every extreme that they name: hash_table sends 8008 // 8 or more ids to every expert. `token_ids`: in every micro-batch the 384 tokens of one device name any expert, through hash_table, at most 96 times; in every micro-batch one expert is named exactly 96 times by the tokens of every device. `segment_ids`: in each micro-batch a device's block holds either one sequence (all 0) or a sequence of 256 tokens (0) followed by one of the rest (1).
All inputs are finite; a program needn't handle non-finite values.
Results may differ from a plain program's by a relative error of at most 0.012.
Values may be sent and summed in bfloat16 or wider, within the bound.
No kernel may reach another device: no remote copies, remote signals or barrier semaphores. Data moves between devices by JAX's collectives and lax.ppermute only.
A program may use at most 192 MiB of HBM per device.

v0:
```python
import jax
import jax.numpy as jnp
from jax import lax
from jax.sharding import PartitionSpec as P

HEADS = 12
HEAD_DIM = 64
epsilon = 1e-05


def normalize(values, gain):
    return values * lax.rsqrt(jnp.mean(values * values, axis=-1, keepdims=True) + epsilon) * gain


def smooth_slope(values):
    sigmoid_part = jax.nn.sigmoid(values)
    return sigmoid_part * (1.0 + values * (1.0 - sigmoid_part))


def split_heads(matrix, head_count):
    return matrix.reshape(matrix.shape[0], head_count, -1).transpose(1, 0, 2)


def merge_heads(tensor):
    return tensor.transpose(1, 0, 2).reshape(tensor.shape[1], -1)


def masked_scores(query_heads, key_heads, allowed, score_scale):
    scores = (
        jnp.einsum("hqd,hkd->hqk", query_heads, key_heads, preferred_element_type=jnp.float32)
        * score_scale
    )
    return jnp.where(allowed[None], scores, -1e30)


def per_device(
    tokens,
    cotangent,
    token_ids,
    hash_table,
    segment_ids,
    query_weight,
    key_weight,
    value_weight,
    output_weight,
    gain_attn,
    gain_ffn,
    expert_in,
    expert_out,
):
    batches = tokens.shape[0]
    length = tokens.shape[1]
    model_width = tokens.shape[2]
    owners = lax.axis_size("expert")
    capacity = 2 * length // owners
    head_count = HEADS
    score_scale = HEAD_DIM ** (-0.5)
    weight_in = expert_in[0]
    weight_out = expert_out[0]
    position = jnp.arange(length, dtype=jnp.int32)
    float_type = jnp.float32
    half_type = jnp.bfloat16
    dense_total = (
        jnp.zeros(query_weight.shape, float_type),
        jnp.zeros(key_weight.shape, float_type),
        jnp.zeros(value_weight.shape, float_type),
        jnp.zeros(output_weight.shape, float_type),
        jnp.zeros(gain_attn.shape, float_type),
        jnp.zeros(gain_ffn.shape, float_type),
    )
    grad_in_sum = jnp.zeros(weight_in.shape, float_type)
    grad_out_sum = jnp.zeros(weight_out.shape, float_type)
    outputs = []
    grads_in = []
    for batch in range(batches):
        inputs_f = tokens[batch].astype(float_type)
        segments = segment_ids[batch]
        allowed = (position[:, None] >= position[None, :]) & (
            segments[:, None] == segments[None, :]
        )
        normed_attn = normalize(inputs_f, gain_attn).astype(half_type)
        query_heads = split_heads(
            jnp.dot(normed_attn, query_weight, preferred_element_type=float_type).astype(half_type),
            head_count,
        )
        key_heads = split_heads(
            jnp.dot(normed_attn, key_weight, preferred_element_type=float_type).astype(half_type),
            head_count,
        )
        value_heads = split_heads(
            jnp.dot(normed_attn, value_weight, preferred_element_type=float_type).astype(half_type),
            head_count,
        )
        scores = masked_scores(query_heads, key_heads, allowed, score_scale)
        row_peak = jnp.max(scores, axis=-1, keepdims=True)
        log_total = row_peak + jnp.log(jnp.sum(jnp.exp(scores - row_peak), axis=-1, keepdims=True))
        probs_low = jnp.exp(scores - log_total).astype(half_type)
        attended = merge_heads(
            jnp.einsum("hqk,hkd->hqd", probs_low, value_heads, preferred_element_type=float_type)
        ).astype(half_type)
        hidden = inputs_f + jnp.dot(attended, output_weight, preferred_element_type=float_type)
        routed = normalize(hidden, gain_ffn).astype(half_type)
        experts = jnp.take(hash_table, token_ids[batch])
        onehot = (experts[:, None] == jnp.arange(owners, dtype=jnp.int32)[None, :]).astype(
            jnp.int32
        )
        rank = jnp.sum((jnp.cumsum(onehot, axis=0, dtype=jnp.int32) - onehot) * onehot, axis=1)
        slot_index = experts * capacity + rank
        packed = jnp.zeros((owners * capacity, model_width), half_type).at[slot_index].set(routed)
        packed = packed.reshape(owners, capacity, model_width)
        received = lax.all_to_all(
            packed, "expert", split_axis=0, concat_axis=0, tiled=True
        ).reshape(owners * capacity, model_width)
        pre_active = jnp.dot(received, weight_in, preferred_element_type=float_type)
        active = jax.nn.silu(pre_active).astype(half_type)
        produced = jnp.dot(active, weight_out, preferred_element_type=float_type).astype(half_type)
        returned = lax.all_to_all(
            produced.reshape(owners, capacity, model_width),
            "expert",
            split_axis=0,
            concat_axis=0,
            tiled=True,
        )
        returned = returned.reshape(owners * capacity, model_width)
        block_out = hidden + jnp.take(returned, slot_index, axis=0).astype(float_type)
        outputs.append(block_out.astype(half_type))
        grad_block = cotangent[batch].astype(float_type)
        grad_result = grad_block.astype(half_type)
        grad_packed = (
            jnp.zeros((owners * capacity, model_width), half_type).at[slot_index].set(grad_result)
        )
        grad_packed = grad_packed.reshape(owners, capacity, model_width)
        grad_recv = lax.all_to_all(grad_packed, "expert", split_axis=0, concat_axis=0, tiled=True)
        grad_recv = grad_recv.reshape(owners * capacity, model_width)
        slope = smooth_slope(pre_active)
        grad_out_sum = grad_out_sum + jnp.dot(
            active.T, grad_recv, preferred_element_type=float_type
        )
        grad_active = jnp.dot(grad_recv, weight_out.T, preferred_element_type=float_type)
        grad_pre = (grad_active * slope).astype(half_type)
        grad_in_sum = grad_in_sum + jnp.dot(received.T, grad_pre, preferred_element_type=float_type)
        grad_rows = jnp.dot(grad_pre, weight_in.T, preferred_element_type=float_type).astype(
            half_type
        )
        grad_back = lax.all_to_all(
            grad_rows.reshape(owners, capacity, model_width),
            "expert",
            split_axis=0,
            concat_axis=0,
            tiled=True,
        )
        grad_routed = jnp.take(
            grad_back.reshape(owners * capacity, model_width), slot_index, axis=0
        ).astype(float_type)
        ignored_ffn, pull_ffn = jax.vjp(normalize, hidden, gain_ffn)
        grad_from_ffn, grad_gain_two = pull_ffn(grad_routed)
        grad_hidden = grad_block + grad_from_ffn
        grad_attn = grad_hidden.astype(half_type)
        grad_output_term = jnp.dot(attended.T, grad_attn, preferred_element_type=float_type)
        grad_mixed = split_heads(
            jnp.dot(grad_attn, output_weight.T, preferred_element_type=float_type).astype(
                half_type
            ),
            head_count,
        )
        scores_again = masked_scores(query_heads, key_heads, allowed, score_scale)
        probs = jnp.exp(scores_again - log_total)
        probs_again = probs.astype(half_type)
        grad_values = jnp.einsum(
            "hqk,hqd->hkd", probs_again, grad_mixed, preferred_element_type=float_type
        ).astype(half_type)
        grad_probs = jnp.einsum(
            "hqd,hkd->hqk", grad_mixed, value_heads, preferred_element_type=float_type
        )
        shared = jnp.sum(probs * grad_probs, axis=-1, keepdims=True)
        grad_scores = (probs * (grad_probs - shared)).astype(half_type)
        grad_queries = (
            jnp.einsum("hqk,hkd->hqd", grad_scores, key_heads, preferred_element_type=float_type)
            * score_scale
        ).astype(half_type)
        grad_keys = (
            jnp.einsum("hqk,hqd->hkd", grad_scores, query_heads, preferred_element_type=float_type)
            * score_scale
        ).astype(half_type)
        grad_queries = merge_heads(grad_queries)
        grad_keys = merge_heads(grad_keys)
        grad_values = merge_heads(grad_values)
        grad_query_term = jnp.dot(normed_attn.T, grad_queries, preferred_element_type=float_type)
        grad_key_term = jnp.dot(normed_attn.T, grad_keys, preferred_element_type=float_type)
        grad_value_term = jnp.dot(normed_attn.T, grad_values, preferred_element_type=float_type)
        grad_normed = (
            jnp.dot(grad_queries, query_weight.T, preferred_element_type=float_type)
            + jnp.dot(grad_keys, key_weight.T, preferred_element_type=float_type)
            + jnp.dot(grad_values, value_weight.T, preferred_element_type=float_type)
        )
        ignored_attn, pull_attn = jax.vjp(normalize, inputs_f, gain_attn)
        grad_from_attn, grad_gain_one = pull_attn(grad_normed)
        grads_in.append((grad_hidden + grad_from_attn).astype(half_type))
        terms = (
            grad_query_term,
            grad_key_term,
            grad_value_term,
            grad_output_term,
            grad_gain_one,
            grad_gain_two,
        )
        dense_total = tuple((total + term for total, term in zip(dense_total, terms)))
    dense_total = lax.psum(
        (
            dense_total[0],
            dense_total[1],
            dense_total[2],
            dense_total[3],
            dense_total[4],
            dense_total[5],
        ),
        ("dp", "expert"),
    )
    expert_in_sum, expert_out_sum = (
        lax.psum(grad_in_sum.astype(jnp.bfloat16), "dp").astype(jnp.float32),
        lax.psum(grad_out_sum.astype(jnp.bfloat16), "dp").astype(jnp.float32),
    )
    return (
        jnp.stack(outputs),
        jnp.stack(grads_in),
        dense_total[0],
        dense_total[1],
        dense_total[2],
        dense_total[3],
        dense_total[4],
        dense_total[5],
        expert_in_sum[None],
        expert_out_sum[None],
    )


def solution(mesh):
    placed = (
        P(None, ("dp", "expert"), None),
        P(None, ("dp", "expert"), None),
        P(None, ("dp", "expert")),
        P(),
        P(None, ("dp", "expert")),
        P(),
        P(),
        P(),
        P(),
        P(),
        P(),
        P("expert", None, None),
        P("expert", None, None),
    )
    return jax.shard_map(
        per_device,
        mesh=mesh,
        in_specs=placed,
        out_specs=(
            P(None, ("dp", "expert"), None),
            P(None, ("dp", "expert"), None),
            P(),
            P(),
            P(),
            P(),
            P(),
            P(),
            P("expert", None, None),
            P("expert", None, None),
        ),
        check_vma=False,
    )
```

profile of v0, /device:TPU:0, one launch (start us, length us, event | category | flops | bytes accessed | tf_op | source)
XLA Modules:
  0.0 789.7 jit_solution(1991907835853382940)
XLA Ops:
  40.1 5.7 all-to-all-start
  63.0 5.8 convolution_convert_fusion
  88.1 9.2 %all-to-all-done.2 = bf16[8,96,768]{2,1,0:T(8,128)(2,1)S(1)} async-done(((bf16[8,96,768]{2,1,0:T(8,128)(2,1)}), bf16[8,96,768]{2,1,0:T(8,128)(2,1)S(1)}, u32[]{:S(2)}, u32[]{:S(2)}) %all-to-all-start.2) | async-done | bytes 1179680 | tf_op jit(solution)/shard_map/all_to_all | solution.py:111
  100.9 12.6 %multiply_convert_fusion.3 = (bf16[768,3072]{1,0:T(8,128)(2,1)}, f32[768,3072]{1,0:T(8,128)}) fusion(bf16[768,768]{1,0:T(8,128)(2,1)} %bitcast.13, bf16[1,768,3072]{2,1,0:T(8,128)(2,1)} %param.28), kind=kOutput, calls=%fused_computation.16 | convolution fusion | flops 3635675136 | bytes 20054016 | tf_op jit(solution)/shard_map/dot_general | solution.py:114
  113.5 8.5 %fusion.12 = f32[768,3072]{1,0:T(8,128)} fusion(bf16[768,768]{1,0:T(8,128)(2,1)S(1)} %bitcast.311, bf16[1,768,3072]{2,1,0:T(8,128)(2,1)} %param.28), kind=kOutput, calls=%fused_computation.40 | convolution fusion | flops 3623878656 | bytes 15335424 | tf_op jit(solution)/shard_map/dot_general | solution.py:114
  126.1 8.8 %multiply_convert_fusion.1 = bf16[768,3072]{1,0:T(8,128)(2,1)S(1)} fusion(f32[768,3072]{1,0:T(8,128)} %get-tuple-element.57, bf16[768,768]{1,0:T(8,128)(2,1)S(1)} %bitcast.314, bf16[1,3072,768]{2,1,0:T(8,128)(2,1)} %param.29), kind=kOutput, calls=%fused_computation.13 | convolution fusion | flops 3645112320 | bytes 20054016 | tf_op jit(solution)/shard_map/dot_general | solution.py:139
  135.0 10.2 %fusion.145 = f32[3072,768]{1,0:T(8,128)} fusion(bf16[768,3072]{1,0:T(8,128)(2,1)} %get-tuple-element.56, bf16[768,768]{1,0:T(8,128)(2,1)S(1)} %bitcast.315), kind=kOutput, calls=%fused_computation.230 | convolution fusion | flops 3623878656 | bytes 15335424 | tf_op jit(solution)/shard_map/dot_general | solution.py:136
  145.2 7.2 fusion.20
  156.9 8.9 %multiply_convert_fusion = bf16[768,3072]{1,0:T(8,128)(2,1)S(1)} fusion(f32[768,3072]{1,0:T(8,128)} %fusion.12, bf16[768,768]{1,0:T(8,128)(2,1)S(1)} %bitcast.316, bf16[1,3072,768]{2,1,0:T(8,128)(2,1)} %param.29), kind=kOutput, calls=%fused_computation.12 | convolution fusion | flops 3645112320 | bytes 20054016 | tf_op jit(solution)/shard_map/dot_general | solution.py:139
  165.8 15.0 %fusion.17 = bf16[1,3072,768]{2,1,0:T(8,128)(2,1)} fusion(f32[3072,768]{1,0:T(8,128)} %fusion.145, bf16[768,768]{1,0:T(8,128)(2,1)S(1)} %bitcast.317, f32[768,3072]{1,0:T(8,128)} %fusion.12), kind=kOutput, calls=%fused_computation.45 | convolution fusion | flops 3640393728 | bytes 24772608 | tf_op jit(solution)/shard_map/dot_general | solution.py:136
  180.9 4.9 fusion.23
  185.7 4.6 all-to-all-start.7
  190.4 11.1 %fusion.29 = bf16[768,768]{1,0:T(8,128)(2,1)} fusion(bf16[1,3072,768]{2,1,0:T(8,128)(2,1)} %param.29, f32[768,3072]{1,0:T(8,128)} %fusion.12), kind=kOutput, calls=%fused_computation.59 | convolution fusion | flops 3636264960 | bytes 15335424 | tf_op jit(solution)/shard_map/dot_general | solution.py:116
  201.4 5.7 all-to-all-done.7
  211.4 10.3 %fusion.144 = f32[768,3072]{1,0:T(8,128)} fusion(bf16[768,768]{1,0:T(8,128)(2,1)} %bitcast.13, bf16[768,3072]{1,0:T(8,128)(2,1)} %copy-done.26), kind=kOutput, calls=%fused_computation.229 | convolution fusion | flops 3623878656 | bytes 15335424 | tf_op jit(solution)/shard_map/dot_general | solution.py:141
  221.8 8.6 %fusion.26 = bf16[768,768]{1,0:T(8,128)(2,1)} fusion(bf16[768,3072]{1,0:T(8,128)(2,1)} %get-tuple-element.56, bf16[1,3072,768]{2,1,0:T(8,128)(2,1)} %param.29), kind=kOutput, calls=%fused_computation.58 | convolution fusion | flops 3624468480 | bytes 10616832 | tf_op jit(solution)/shard_map/dot_general | solution.py:116
  234.9 11.5 %fusion.16 = bf16[1,768,3072]{2,1,0:T(8,128)(2,1)} fusion(f32[768,3072]{1,0:T(8,128)} %fusion.144, bf16[768,768]{1,0:T(8,128)(2,1)} %bitcast.312, bf16[768,3072]{1,0:T(8,128)(2,1)} %copy-done.92), kind=kOutput, calls=%fused_computation.44 | convolution fusion | flops 3628597248 | bytes 20054016 | tf_op jit(solution)/shard_map/dot_general | solution.py:141
  249.7 4.4 gather_fusion.3
  277.9 5.6 multiply_reduce_fusion.1
  325.5 46.7 %all-reduce = (f32[768]{0:T(1024)}, f32[768]{0:T(1024)}) all-reduce(f32[768]{0:T(1024)} %add.207, f32[768]{0:T(1024)} %add.208), channel_id=1, replica_groups=mesh['dp'=4,'expert'=8] {'dp','expert'}, use_global_device_ids=true, to_apply=%region_30.33 | all-reduce | flops 1536 | bytes 12288 | tf_op jit(solution)/shard_map/psum | solution.py:208
  378.5 196.6 %all-reduce.8.cloned.1.call-done = (bf16[1,768,3072]{2,1,0:T(8,128)(2,1)}, bf16[1,3072,768]{2,1,0:T(8,128)(2,1)}) async-done(((bf16[1,768,3072]{2,1,0:T(8,128)(2,1)}, bf16[1,3072,768]{2,1,0:T(8,128)(2,1)}), (bf16[1,768,3072]{2,1,0:T(8,128)(2,1)}, bf16[1,3072,768]{2,1,0:T(8,128)(2,1)})) %all-reduce.8.cloned.1.call-update) | async-done | bytes 9437200 | tf_op jit(solution)/shard_map/psum | solution.py:220
  575.1 7.5 broadcast_in_dim.117
  582.6 4.9 broadcast_in_dim.119
  587.5 185.4 %all-reduce.6.cloned.1.call-done = (f32[768,768]{1,0:T(8,128)}, f32[768,768]{1,0:T(8,128)}, f32[768,768]{1,0:T(8,128)}, f32[768,768]{1,0:T(8,128)}) async-done(((f32[768,768]{1,0:T(8,128)}, f32[768,768]{1,0:T(8,128)}, f32[768,768]{1,0:T(8,128)}, f32[768,768]{1,0:T(8,128)}), (f32[768,768]{1,0:T(8,128)}, f32[768,768]{1,0:T(8,128)}, f32[768,768]{1,0:T(8,128)}, ...) | async-done | bytes 9437200 | tf_op jit(solution)/shard_map/psum | solution.py:208
  (317 shorter events, 174.5 us)
Async XLA Ops:
  8.9 36.9 %copy-start.79 = (f32[384]{0:T(512)}, f32[384]{0:T(512)S(1)}, u32[]{:S(2)}) copy-start(f32[384]{0:T(512)S(1)} %get-tuple-element.23) | copy-start | bytes 4612
  9.5 8.2 %copy-start.69 = (f32[384]{0:T(512)}, f32[384]{0:T(512)S(1)}, u32[]{:S(2)}) copy-start(f32[384]{0:T(512)S(1)} %fusion.115) | copy-start | bytes 4612
  31.7 8.4 %copy-start.73 = (f32[384]{0:T(512)}, f32[384]{0:T(512)S(1)}, u32[]{:S(2)}) copy-start(f32[384]{0:T(512)S(1)} %fusion.116) | copy-start | bytes 4612
  40.1 36.0 %all-to-all-start = ((bf16[8,96,768]{2,1,0:T(8,128)(2,1)}), bf16[8,96,768]{2,1,0:T(8,128)(2,1)}, u32[]{:S(2)}, u32[]{:S(2)}) async-start(bf16[8,96,768]{2,1,0:T(8,128)(2,1)} %bitcast.300), calls=%async_computation | async-start | bytes 2359296 | tf_op jit(solution)/shard_map/all_to_all | solution.py:111
  51.3 11.7 %copy-start.40 = (pred[384,384]{0,1:T(8,128)(4,1)}, pred[384,384]{0,1:T(8,128)(4,1)S(1)}, u32[]{:S(2)}) copy-start(pred[384,384]{0,1:T(8,128)(4,1)S(1)} %fusion.96) | copy-start | bytes 442372
  60.4 8.4 %copy-start.63 = (f32[12,384]{1,0:T(8,128)}, f32[12,384]{1,0:T(8,128)S(1)}, u32[]{:S(2)}) copy-start(f32[12,384]{1,0:T(8,128)S(1)} %log_add_fusion) | copy-start | bytes 55300
  76.1 21.2 %all-to-all-start.2 = ((bf16[8,96,768]{2,1,0:T(8,128)(2,1)}), bf16[8,96,768]{2,1,0:T(8,128)(2,1)S(1)}, u32[]{:S(2)}, u32[]{:S(2)}) async-start(bf16[8,96,768]{2,1,0:T(8,128)(2,1)} %bitcast.31), calls=%async_computation.2 | async-start | bytes 2359296 | tf_op jit(solution)/shard_map/all_to_all | solution.py:111
  97.3 16.2 %copy-start.54 = (bf16[8,96,768]{2,1,0:T(8,128)(2,1)}, bf16[8,96,768]{2,1,0:T(8,128)(2,1)S(1)}, u32[]{:S(2)}) copy-start(bf16[8,96,768]{2,1,0:T(8,128)(2,1)S(1)} %all-to-all-done.2) | copy-start | bytes 3538948
  97.3 24.7 %all-to-all-start.4 = ((bf16[8,96,768]{2,1,0:T(8,128)(2,1)}), bf16[8,96,768]{2,1,0:T(8,128)(2,1)S(1)}, u32[]{:S(2)}, u32[]{:S(2)}) async-start(bf16[8,96,768]{2,1,0:T(8,128)(2,1)} %bitcast.37), calls=%async_computation.4 | async-start | bytes 2359296 | tf_op jit(solution)/shard_map/all_to_all | solution.py:133
  122.0 30.4 %all-to-all-start.6 = ((bf16[8,96,768]{2,1,0:T(8,128)(2,1)}), bf16[8,96,768]{2,1,0:T(8,128)(2,1)S(1)}, u32[]{:S(2)}, u32[]{:S(2)}) async-start(bf16[8,96,768]{2,1,0:T(8,128)(2,1)} %bitcast.55), calls=%async_computation.6 | async-start | bytes 2359296 | tf_op jit(solution)/shard_map/all_to_all | solution.py:133
  134.9 10.3 %copy-start.26 = (bf16[768,3072]{1,0:T(8,128)(2,1)}, bf16[768,3072]{1,0:T(8,128)(2,1)S(1)}, u32[]{:S(2)}) copy-start(bf16[768,3072]{1,0:T(8,128)(2,1)S(1)} %multiply_convert_fusion.1) | copy-start | bytes 14155780
  152.4 33.3 %all-to-all-start.5 = ((bf16[8,96,768]{2,1,0:T(8,128)(2,1)}), bf16[8,96,768]{2,1,0:T(8,128)(2,1)S(1)}, u32[]{:S(2)}, u32[]{:S(2)}) async-start(bf16[8,96,768]{2,1,0:T(8,128)(2,1)} %bitcast.319), calls=%async_computation.5 | async-start | bytes 2359296 | tf_op jit(solution)/shard_map/all_to_all | solution.py:145
  156.8 24.0 %slice-start.4 = ((s8[4718592]{0:T(1024)(128)(4,1)}), s8[4194304]{0:T(1024)(128)(4,1)S(1)}, s32[]{:S(2)}) async-start(s8[4718592]{0:T(1024)(128)(4,1)} %bitcast.331), calls=%async_computation.14 | async-start | bytes 8388608
  165.8 15.0 %copy-start.92 = (bf16[768,3072]{1,0:T(8,128)(2,1)}, bf16[768,3072]{1,0:T(8,128)(2,1)S(1)}, u32[]{:S(2)}) copy-start(bf16[768,3072]{1,0:T(8,128)(2,1)S(1)} %multiply_convert_fusion) | copy-start | bytes 14155780
  165.8 15.0 %slice-start.5 = ((s8[4718592]{0:T(1024)(128)(4,1)}), s8[524288]{0:T(1024)(128)(4,1)S(1)}, s32[]{:S(2)}) async-start(s8[4718592]{0:T(1024)(128)(4,1)} %bitcast.331), calls=%async_computation.15 | async-start | bytes 1048576
  185.7 21.4 %all-to-all-start.7 = ((bf16[8,96,768]{2,1,0:T(8,128)(2,1)}), bf16[8,96,768]{2,1,0:T(8,128)(2,1)S(1)}, u32[]{:S(2)}, u32[]{:S(2)}) async-start(bf16[8,96,768]{2,1,0:T(8,128)(2,1)} %bitcast.320), calls=%async_computation.7 | async-start | bytes 2359296 | tf_op jit(solution)/shard_map/all_to_all | solution.py:145
  207.2 23.2 %all-to-all-start.3 = ((bf16[8,96,768]{2,1,0:T(8,128)(2,1)}), bf16[8,96,768]{2,1,0:T(8,128)(2,1)}, u32[]{:S(2)}, u32[]{:S(2)}) async-start(bf16[8,96,768]{2,1,0:T(8,128)(2,1)} %bitcast.318), calls=%async_computation.3 | async-start | bytes 2359296 | tf_op jit(solution)/shard_map/all_to_all | solution.py:117
  230.4 30.2 %all-to-all-start.1 = ((bf16[8,96,768]{2,1,0:T(8,128)(2,1)}), bf16[8,96,768]{2,1,0:T(8,128)(2,1)}, u32[]{:S(2)}, u32[]{:S(2)}) async-start(bf16[8,96,768]{2,1,0:T(8,128)(2,1)} %bitcast.313), calls=%async_computation.1 | async-start | bytes 2359296 | tf_op jit(solution)/shard_map/all_to_all | solution.py:117
  234.6 340.4 %all-reduce.8.cloned.1.call-start = ((), (), s32[]{:S(2)}) async-start(), calls=%async_computation.9 | async-start | bytes 18874368 | tf_op jit(solution)/shard_map/psum | solution.py:220
  246.4 526.4 %all-reduce.6.cloned.1.call-start = ((), (), s32[]{:S(2)}) async-start(), calls=%async_computation.8 | async-start | bytes 18874368 | tf_op jit(solution)/shard_map/psum | solution.py:208
  277.9 5.7 slice-start
  288.2 7.2 slice-start.2
  321.8 53.0 %copy-start.80 = (f32[384]{0:T(512)S(1)}, f32[384]{0:T(512)}, u32[]{:S(2)}) copy-start(f32[384]{0:T(512)} %copy-done.79) | copy-start | bytes 4612
  575.1 7.5 copy-start.25
  (85 other events, 202.0 us)
Sparse Core Ops, SparseCore 0:
  246.5 328.4 all-reduce.7
  581.9 190.9 all-reduce.5
where the time goes:
time: 799 us; the launch traced here: 790 us
  waiting for transfers between devices  397 us (50%)
  matrix products  184 us (23%)
  local copies, waits for them, and re-layouts  61.3 us (8%)
  other arithmetic  49.6 us (6%)
  blocking collectives  46.7 us (6%)
  starting transfers between devices  35.6 us (4%)
  between operations  15.4 us (2%)
    psum x1, waiting for transfers between devices, per_device(): lax.psum(grad_in_sum.astype(jnp.bfloat16), 'dp').astype(jnp.float32)  197 us
    psum x1, waiting for transfers between devices, per_device(): lax.psum((dense_total[0], dense_total[1], dense_total[2], dense_total[3],...  185 us
    psum x1, blocking collectives, per_device(): lax.psum((dense_total[0], dense_total[1], dense_total[2], dense_total[3],...  46.7 us
    dot_general x2, matrix products, per_device(): jnp.dot(active.T, grad_recv, preferred_element_type=float_type)  25.3 us
    dot_general x2, matrix products, per_device(): jnp.dot(received.T, grad_pre, preferred_element_type=float_type)  21.9 us
    dot_general x2, matrix products, per_device(): pre_active = jnp.dot(received, weight_in, preferred_element_type=float_type)  21.1 us
    unnamed x202, local copies, waits for them, and re-layouts  20.3 us
    dot_general x2, matrix products, per_device(): jnp.dot(active, weight_out, preferred_element_type=float_type)  19.7 us
  transfers between devices with their start and end apart: 10, of which 4 were waited for; matrix products, arithmetic and copies ran while one was open for 31% of the time, Pallas kernels for 0%

commit v1 on v0

--- a/solution.py
+++ b/solution.py
@@ -205,17 +205,16 @@
             grad_gain_two,
         )
         dense_total = tuple((total + term for total, term in zip(dense_total, terms)))
-    dense_total = lax.psum(
-        (
-            dense_total[0],
-            dense_total[1],
-            dense_total[2],
-            dense_total[3],
-            dense_total[4],
-            dense_total[5],
-        ),
-        ("dp", "expert"),
-    )
+    dense_total = (
+        dense_total[0],
+        dense_total[1],
+        dense_total[2],
+        dense_total[3],
+        dense_total[4],
+        dense_total[5],
+    )
+    for over in ("expert", "dp"):
+        dense_total = lax.psum(dense_total, over)
     expert_in_sum, expert_out_sum = (
         lax.psum(grad_in_sum.astype(jnp.bfloat16), "dp").astype(jnp.float32),
         lax.psum(grad_out_sum.astype(jnp.bfloat16), "dp").astype(jnp.float32),

time: 799 us -> 1110 us (1.39)
  waiting for transfers between devices: 397 us -> 734 us
  blocking collectives: 46.7 us -> 27.6 us
    psum x1 -> x2, waiting for transfers between devices: 185 us -> 424 us  [per_device(): dense_total = lax.psum(dense_total, over)]
    psum x1, waiting for transfers between devices: 197 us -> 284 us  [per_device(): lax.psum(grad_in_sum.astype(jnp.bfloat16), 'dp').astype(jnp.float32)]
    psum x1 -> x2, blocking collectives: 46.7 us -> 27.6 us  [per_device(): dense_total = lax.psum(dense_total, over)]
  transfers between devices with their start and end apart: 10 -> 11, of which waited for: 4 -> 8; matrix products, arithmetic and copies ran while one was open for 31% -> 17% of each run, Pallas kernels for 0% -> 0%
where the time goes in v1:
time: 1110 us; the launch traced here: 1100 us
  waiting for transfers between devices  734 us (66%)
  matrix products  177 us (16%)
  local copies, waits for them, and re-layouts  64.9 us (6%)
  other arithmetic  50.8 us (5%)
  starting transfers between devices  34 us (3%)
  blocking collectives  27.6 us (2%)
  between operations  15.1 us (1%)
    psum x2, waiting for transfers between devices, per_device(): dense_total = lax.psum(dense_total, over)  424 us
    psum x1, waiting for transfers between devices, per_device(): lax.psum(grad_in_sum.astype(jnp.bfloat16), 'dp').astype(jnp.float32)  284 us
    psum x2, blocking collectives, per_device(): dense_total = lax.psum(dense_total, over)  27.6 us
  transfers between devices with their start and end apart: 11, of which 8 were waited for; matrix products, arithmetic and copies ran while one was open for 17% of the time, Pallas kernels for 0%

profile of v1, /device:TPU:0, one launch (start us, length us, event | category | flops | bytes accessed | tf_op | source)
XLA Modules:
  0.0 1103.7 jit_solution(1266242767041159547)
XLA Ops:
  40.7 5.4 all-to-all-start
  86.5 12.6 %multiply_convert_fusion.3 = (bf16[768,3072]{1,0:T(8,128)(2,1)}, f32[768,3072]{1,0:T(8,128)}) fusion(bf16[768,768]{1,0:T(8,128)(2,1)} %bitcast.13, bf16[1,768,3072]{2,1,0:T(8,128)(2,1)} %param.28), kind=kOutput, calls=%fused_computation.16 | convolution fusion | flops 3635675136 | bytes 20054016 | tf_op jit(solution)/shard_map/dot_general | solution.py:114
  106.9 10.2 multiply_convert_fusion.1
  117.1 6.5 all-to-all-done.2
  128.5 8.7 fusion.12
  137.2 7.2 fusion.20
  148.8 8.9 multiply_convert_fusion
  159.8 7.2 fusion.23
  171.3 11.3 %fusion.29 = bf16[768,768]{1,0:T(8,128)(2,1)} fusion(bf16[1,3072,768]{2,1,0:T(8,128)(2,1)} %param.29, f32[768,3072]{1,0:T(8,128)} %fusion.12), kind=kOutput, calls=%fused_computation.59 | convolution fusion | flops 3636264960 | bytes 15335424 | tf_op jit(solution)/shard_map/dot_general | solution.py:116
  182.6 5.5 all-to-all-done.7
  193.4 8.6 fusion.26
  202.0 8.2 all-to-all-done.3
  242.9 5.9 multiply_reduce_fusion
  261.4 5.7 multiply_reduce_fusion.1
  287.9 6.4 fusion.144
  294.3 9.6 fusion.145
  303.8 8.1 fusion.16
  312.0 9.3 fusion.17
  321.4 107.6 %all-reduce.9.cloned.1.call-done = (f32[768,768]{1,0:T(8,128)}, f32[768,768]{1,0:T(8,128)}, f32[768,768]{1,0:T(8,128)}, f32[768,768]{1,0:T(8,128)}) async-done(((f32[768,768]{1,0:T(8,128)}, f32[768,768]{1,0:T(8,128)}, f32[768,768]{1,0:T(8,128)}, f32[768,768]{1,0:T(8,128)}), (f32[768,768]{1,0:T(8,128)}, f32[768,768]{1,0:T(8,128)}, f32[768,768]{1,0:T(8,128)}, ...) | async-done | bytes 9437200 | tf_op jit(solution)/shard_map/psum | solution.py:217
  440.2 14.5 %all-reduce = (f32[768]{0:T(1024)}, f32[768]{0:T(1024)}) all-reduce(f32[768]{0:T(1024)} %add.219, f32[768]{0:T(1024)} %add.220), channel_id=1, replica_groups=mesh['dp'=4,'expert'=8] {'expert'}, use_global_device_ids=true, to_apply=%region_34.37 | all-reduce | flops 1536 | bytes 12288 | tf_op jit(solution)/shard_map/psum | solution.py:217
  454.6 13.1 %all-reduce.2 = (f32[768]{0:T(1024)}, f32[768]{0:T(1024)}) all-reduce(f32[768]{0:T(1024)} %get-tuple-element.28, f32[768]{0:T(1024)} %get-tuple-element.29), channel_id=1, replica_groups=mesh['dp'=4,'expert'=8] {'dp'}, use_global_device_ids=true, to_apply=%region_35.38 | all-reduce | flops 1536 | bytes 12288 | tf_op jit(solution)/shard_map/psum | solution.py:217
  474.0 284.3 %all-reduce.13.cloned.1.call-done = (bf16[1,768,3072]{2,1,0:T(8,128)(2,1)}, bf16[1,3072,768]{2,1,0:T(8,128)(2,1)}) async-done(((bf16[1,768,3072]{2,1,0:T(8,128)(2,1)}, bf16[1,3072,768]{2,1,0:T(8,128)(2,1)}), (bf16[1,768,3072]{2,1,0:T(8,128)(2,1)}, bf16[1,3072,768]{2,1,0:T(8,128)(2,1)})) %all-reduce.13.cloned.1.call-update) | async-done | bytes 9437200 | tf_op jit(solution)/shard_map/psum | solution.py:219
  758.3 7.5 broadcast_in_dim.117
  770.3 316.8 %all-reduce.11.cloned.1.call-done = (f32[768,768]{1,0:T(8,128)}, f32[768,768]{1,0:T(8,128)}, f32[768,768]{1,0:T(8,128)}, f32[768,768]{1,0:T(8,128)}) async-done(((f32[768,768]{1,0:T(8,128)}, f32[768,768]{1,0:T(8,128)}, f32[768,768]{1,0:T(8,128)}, f32[768,768]{1,0:T(8,128)}), (f32[768,768]{1,0:T(8,128)}, f32[768,768]{1,0:T(8,128)}, f32[768,768]{1,0:T(8,128)}, ...) | async-done | bytes 9437200 | tf_op jit(solution)/shard_map/psum | solution.py:217
  (316 shorter events, 199.6 us)
Async XLA Ops:
  8.9 37.1 %copy-start.74 = (f32[384]{0:T(512)}, f32[384]{0:T(512)S(1)}, u32[]{:S(2)}) copy-start(f32[384]{0:T(512)S(1)} %get-tuple-element.23) | copy-start | bytes 4612
  9.5 8.8 copy-start.68
  36.7 13.7 %copy-start.81 = (s32[384]{0:T(512)}, s32[384]{0:T(512)S(1)}, u32[]{:S(2)}) copy-start(s32[384]{0:T(512)S(1)} %get-tuple-element.43) | copy-start | bytes 4612
  40.7 41.7 %all-to-all-start = ((bf16[8,96,768]{2,1,0:T(8,128)(2,1)}), bf16[8,96,768]{2,1,0:T(8,128)(2,1)}, u32[]{:S(2)}, u32[]{:S(2)}) async-start(bf16[8,96,768]{2,1,0:T(8,128)(2,1)} %bitcast.301), calls=%async_computation | async-start | bytes 2359296 | tf_op jit(solution)/shard_map/all_to_all | solution.py:111
  55.2 17.3 %copy-start.39 = (pred[384,384]{0,1:T(8,128)(4,1)}, pred[384,384]{0,1:T(8,128)(4,1)S(1)}, u32[]{:S(2)}) copy-start(pred[384,384]{0,1:T(8,128)(4,1)S(1)} %fusion.96) | copy-start | bytes 442372
  64.3 8.2 copy-start.63
  68.7 10.4 copy-start.84
  82.3 21.0 %all-to-all-start.4 = ((bf16[8,96,768]{2,1,0:T(8,128)(2,1)}), bf16[8,96,768]{2,1,0:T(8,128)(2,1)S(1)}, u32[]{:S(2)}, u32[]{:S(2)}) async-start(bf16[8,96,768]{2,1,0:T(8,128)(2,1)} %bitcast.37), calls=%async_computation.4 | async-start | bytes 2359296 | tf_op jit(solution)/shard_map/all_to_all | solution.py:133
  103.3 20.3 %all-to-all-start.2 = ((bf16[8,96,768]{2,1,0:T(8,128)(2,1)}), bf16[8,96,768]{2,1,0:T(8,128)(2,1)S(1)}, u32[]{:S(2)}, u32[]{:S(2)}) async-start(bf16[8,96,768]{2,1,0:T(8,128)(2,1)} %bitcast.31), calls=%async_computation.2 | async-start | bytes 2359296 | tf_op jit(solution)/shard_map/all_to_all | solution.py:111
  123.6 13.5 %slice-start.4 = ((s8[4718592]{0:T(1024)(128)(4,1)}), s8[524288]{0:T(1024)(128)(4,1)S(1)}, s32[]{:S(2)}) async-start(s8[4718592]{0:T(1024)(128)(4,1)} %bitcast.302), calls=%async_computation.15 | async-start | bytes 1048576
  123.7 21.6 %all-to-all-start.6 = ((bf16[8,96,768]{2,1,0:T(8,128)(2,1)}), bf16[8,96,768]{2,1,0:T(8,128)(2,1)}, u32[]{:S(2)}, u32[]{:S(2)}) async-start(bf16[8,96,768]{2,1,0:T(8,128)(2,1)} %bitcast.55), calls=%async_computation.6 | async-start | bytes 2359296 | tf_op jit(solution)/shard_map/all_to_all | solution.py:133
  128.5 8.7 slice-start.5
  145.3 21.7 %all-to-all-start.5 = ((bf16[8,96,768]{2,1,0:T(8,128)(2,1)}), bf16[8,96,768]{2,1,0:T(8,128)(2,1)S(1)}, u32[]{:S(2)}, u32[]{:S(2)}) async-start(bf16[8,96,768]{2,1,0:T(8,128)(2,1)} %bitcast.39), calls=%async_computation.5 | async-start | bytes 2359296 | tf_op jit(solution)/shard_map/all_to_all | solution.py:145
  167.0 21.1 %all-to-all-start.7 = ((bf16[8,96,768]{2,1,0:T(8,128)(2,1)}), bf16[8,96,768]{2,1,0:T(8,128)(2,1)S(1)}, u32[]{:S(2)}, u32[]{:S(2)}) async-start(bf16[8,96,768]{2,1,0:T(8,128)(2,1)} %bitcast.320), calls=%async_computation.7 | async-start | bytes 2359296 | tf_op jit(solution)/shard_map/all_to_all | solution.py:145
  189.1 21.1 %all-to-all-start.3 = ((bf16[8,96,768]{2,1,0:T(8,128)(2,1)}), bf16[8,96,768]{2,1,0:T(8,128)(2,1)}, u32[]{:S(2)}, u32[]{:S(2)}) async-start(bf16[8,96,768]{2,1,0:T(8,128)(2,1)} %bitcast.319), calls=%async_computation.3 | async-start | bytes 2359296 | tf_op jit(solution)/shard_map/all_to_all | solution.py:117
  210.2 22.2 %all-to-all-start.1 = ((bf16[8,96,768]{2,1,0:T(8,128)(2,1)}), bf16[8,96,768]{2,1,0:T(8,128)(2,1)S(1)}, u32[]{:S(2)}, u32[]{:S(2)}) async-start(bf16[8,96,768]{2,1,0:T(8,128)(2,1)} %bitcast.318), calls=%async_computation.1 | async-start | bytes 2359296 | tf_op jit(solution)/shard_map/all_to_all | solution.py:117
  213.8 215.2 %all-reduce.9.cloned.1.call-start = ((), (), s32[]{:S(2)}) async-start(), calls=%async_computation.8 | async-start | bytes 18874368 | tf_op jit(solution)/shard_map/psum | solution.py:217
  239.2 18.5 %copy-start.7 = (f32[384,768]{1,0:T(8,128)}, f32[384,768]{1,0:T(8,128)S(1)}, u32[]{:S(2)}) copy-start(f32[384,768]{1,0:T(8,128)S(1)} %get-tuple-element.48) | copy-start | bytes 3538948
  287.8 470.5 %all-reduce.13.cloned.1.call-start = ((), (), s32[]{:S(2)}) async-start(), calls=%async_computation.10 | async-start | bytes 18874368 | tf_op jit(solution)/shard_map/psum | solution.py:219
  294.2 9.6 copy-start.54
  294.3 17.7 %slice-start.6 = ((s8[9437184]{0:T(1024)(128)(4,1)}), s8[4194304]{0:T(1024)(128)(4,1)S(1)}, s32[]{:S(2)}) async-start(s8[9437184]{0:T(1024)(128)(4,1)} %bitcast.331), calls=%async_computation.17 | async-start | bytes 8388608
  294.3 17.7 %slice-start.7 = ((s8[9437184]{0:T(1024)(128)(4,1)}), s8[4194304]{0:T(1024)(128)(4,1)S(1)}, s32[]{:S(2)}) async-start(s8[9437184]{0:T(1024)(128)(4,1)} %bitcast.331), calls=%async_computation.18 | async-start | bytes 8388608
  321.3 765.8 %all-reduce.11.cloned.1.call-start = ((), (), s32[]{:S(2)}) async-start(), calls=%async_computation.9 | async-start | bytes 18874368 | tf_op jit(solution)/shard_map/psum | solution.py:217
  436.4 33.9 %copy-start.75 = (f32[384]{0:T(512)S(1)}, f32[384]{0:T(512)}, u32[]{:S(2)}) copy-start(f32[384]{0:T(512)} %copy-done.74) | copy-start | bytes 4612
  (83 other events, 244.9 us)
Sparse Core Ops, SparseCore 0:
  287.9 141.0 all-reduce.8
  432.4 325.9 all-reduce.12
  761.4 325.6 all-reduce.10
